TPU v7x, 32 devices: a whole 2x2x4 slice. The times are simulated.
32 devices in a mesh: horiz: 8 (over y, x, core), lev: 4 (over z).
Axes of the slice: x: 2, y: 2, z: 4, core: 2. Of those that a mesh axis runs over, the one named last changes fastest.
Arguments:
- source_state: bfloat16 [5, 68, 32768], P(None, 'lev', 'horiz'), may hold values from -6 to 6
- intersection: int32 [40], P('horiz'), may hold values from 0 to 7, as said below
- index_map: int32 [40, 512], P('horiz'), may hold values from 0 to 4095
- blocks: bfloat16 [40, 512, 2048], P('horiz'), may hold values from -0.125 to 0.125
- bracket: int32 [127, 16384], P(None, ('horiz', 'lev')), may hold values from 0 to 66
- fraction: float32 [127, 16384], P(None, ('horiz', 'lev')), may hold values from 0 to 1
Outputs:
- target_state: bfloat16 [5, 127, 16384], P(None, None, ('horiz', 'lev'))
Inputs may be any that keep to these rules, and one draw needn't show every extreme that they name: For every target group g, intersection[g * 5] to intersection[g * 5 + 4] are the groups g - 2 to g + 2 modulo 8, each once, in some order.
All inputs are finite; a program needn't handle non-finite values.
Results may differ from a plain program's by a relative error of at most 0.0049.
Values may be sent and summed in bfloat16 or wider, within the bound.
A program may use at most 64 MiB of HBM per device.

v0:
```python
import jax
import jax.numpy as jnp
from jax import lax
from jax.sharding import PartitionSpec as P


def shifted(block, axis, distance):
    devices = range(lax.axis_size(axis))
    route = [((i - distance) % len(devices), i) for i in devices]
    return lax.ppermute(block, axis, route)


def select_cells(tile, wanted):
    cell_ids = jnp.arange(tile.shape[1], dtype=jnp.int32)[:, None]
    picker = (cell_ids == wanted[None, :]).astype(jnp.bfloat16)
    return jnp.dot(tile, picker, preferred_element_type=jnp.float32).astype(jnp.bfloat16)


def local(source_state, intersection, index_map, blocks, bracket, fraction):
    fields, level_slab, tile_cells = source_state.shape
    stacked = source_state.reshape(fields * level_slab, tile_cells)
    groups = lax.axis_size("horiz")
    block_count = intersection.shape[0]
    depth = (block_count - 1) // 2
    own_group = lax.axis_index("horiz")
    position = (intersection - own_group + depth) % groups
    collected = []
    for offset in range(-depth, depth + 1):
        wanted_group = (own_group + offset) % groups
        matched = intersection == wanted_group
        request = jnp.sum(jnp.where(matched[:, None], index_map, 0), axis=0)
        if offset == 0:
            collected.append(select_cells(stacked, request))
        else:
            incoming = shifted(request, "horiz", offset)
            outgoing = select_cells(stacked, incoming)
            collected.append(shifted(outgoing, "horiz", -offset))
    by_offset = jnp.stack(collected)
    pieces = [
        lax.dynamic_index_in_dim(by_offset, position[block_slot], 0, keepdims=False)
        for block_slot in range(block_count)
    ]
    chosen = jnp.concatenate(pieces, axis=1)
    weights_flat = blocks.reshape(-1, blocks.shape[2])
    horizontal = jnp.dot(chosen, weights_flat, preferred_element_type=jnp.float32).astype(
        jnp.bfloat16
    )
    horizontal = horizontal.reshape(fields, level_slab, blocks.shape[2])
    level_total = level_slab * lax.axis_size("lev")
    level_ids = jnp.arange(level_total, dtype=jnp.int32)[None, :, None]
    lower_hit = level_ids == bracket[:, None, :]
    upper_hit = level_ids == bracket[:, None, :] + 1
    upper_share = fraction[:, None, :]
    interp = jnp.where(lower_hit, 1.0 - upper_share, 0.0) + jnp.where(upper_hit, upper_share, 0.0)
    widened = lax.all_to_all(horizontal, "lev", split_axis=2, concat_axis=1, tiled=True).astype(
        jnp.float32
    )
    mixed = jnp.einsum("jlc,flc->fjc", interp, widened, precision=lax.Precision.HIGHEST)
    return mixed.astype(jnp.bfloat16)


def solution(mesh):
    in_specs = (
        P(None, "lev", "horiz"),
        P("horiz"),
        P("horiz", None),
        P("horiz", None, None),
        P(None, ("horiz", "lev")),
        P(None, ("horiz", "lev")),
    )
    out_specs = P(None, None, ("horiz", "lev"))
    return jax.shard_map(local, mesh=mesh, in_specs=in_specs, out_specs=out_specs, check_vma=False)
```

profile of v0, /device:TPU:2, one launch (start us, length us, event | category | flops | bytes accessed | tf_op | source)
XLA Modules:
  0.0 84.0 jit_solution(5691113030933345913)
XLA Ops:
  0.0 0.7 broadcast_compare_fusion.1
  0.7 0.8 select_reduce_fusion
  1.5 0.1 collective-permute-start.2
  1.6 2.4 %collective-permute-start = (s32[512]{0:T(512)S(1)}, s32[512]{0:T(512)S(1)}, u32[]{:S(2)}, u32[]{:S(2)}) collective-permute-start(s32[512]{0:T(512)S(1)} %get-tuple-element.8), channel_id=1, source_target_pairs={{8,0},{12,4},{16,8},{20,12},{24,16},{28,20},{0,24},{4,28},{9,1},{1... | collective-permute-start | bytes 6152 | tf_op jit(solution)/shard_map/ppermute | solution.py:10
  4.0 0.0 collective-permute-start.4
  4.0 0.7 collective-permute-start.6
  4.7 0.7 and_select_fusion
  5.4 0.7 fusion.38
  12.4 1.4 %reshape.25 = bf16[85,4096]{1,0:T(8,128)(2,1)S(1)} reshape(bf16[5,17,4096]{2,1,0:T(8,128)(2,1)} %param.6) | data formatting | bytes 1392640 | tf_op jit(solution)/shard_map/reshape | solution.py:21
  17.1 0.0 collective-permute-done.2
  17.1 0.0 slice-start
  17.1 1.5 %fusion.31 = bf16[85,512]{1,0:T(8,128)(2,1)S(1)} fusion(bf16[85,4096]{1,0:T(8,128)(2,1)S(1)} %reshape.25, s32[512]{0:T(512)S(1)} %collective-permute-done.2), kind=kOutput, calls=%fused_computation.35 | convolution fusion | flops 358656512 | bytes 785408 | tf_op jit(solution)/shard_map/dot_general | solution.py:16
  18.6 0.0 slice-start.1
  18.6 1.1 %collective-permute-start.3 = (bf16[85,512]{1,0:T(8,128)(2,1)S(1)}, bf16[85,512]{1,0:T(8,128)(2,1)S(1)}, u32[]{:S(2)}, u32[]{:S(2)}) collective-permute-start(bf16[85,512]{1,0:T(8,128)(2,1)S(1)} %fusion.31), channel_id=1, source_target_pairs={{28,0},{0,4},{4,8},{8,12},{12,16},{16,20},{20,24},{24,28},{29,1},{... | collective-permute-start | bytes 261128 | tf_op jit(solution)/shard_map/ppermute | solution.py:10
  19.7 0.0 collective-permute-done
  19.7 1.5 %fusion.30 = bf16[85,512]{1,0:T(8,128)(2,1)S(1)} fusion(bf16[85,4096]{1,0:T(8,128)(2,1)S(1)} %reshape.25, s32[512]{0:T(512)S(1)} %collective-permute-done), kind=kOutput, calls=%fused_computation.34 | convolution fusion | flops 358656512 | bytes 785408 | tf_op jit(solution)/shard_map/dot_general | solution.py:16
  21.2 1.6 %collective-permute-start.1 = (bf16[85,512]{1,0:T(8,128)(2,1)S(1)}, bf16[85,512]{1,0:T(8,128)(2,1)S(1)}, u32[]{:S(2)}, u32[]{:S(2)}) collective-permute-start(bf16[85,512]{1,0:T(8,128)(2,1)S(1)} %fusion.30), channel_id=1, source_target_pairs={{24,0},{28,4},{0,8},{4,12},{8,16},{12,20},{16,24},{20,28},{25,1},{... | collective-permute-start | bytes 261128 | tf_op jit(solution)/shard_map/ppermute | solution.py:10
  22.9 0.0 collective-permute-done.4
  22.9 1.5 %fusion.34 = bf16[85,512]{1,0:T(8,128)(2,1)S(1)} fusion(bf16[85,4096]{1,0:T(8,128)(2,1)S(1)} %reshape.25, s32[512]{0:T(512)S(1)} %collective-permute-done.4), kind=kOutput, calls=%fused_computation.38 | convolution fusion | flops 358656512 | bytes 785408 | tf_op jit(solution)/shard_map/dot_general | solution.py:16
  24.3 0.0 slice-start.2
  24.3 0.1 collective-permute-start.5
  24.5 0.0 collective-permute-done.6
  24.5 1.5 %fusion.35 = bf16[85,512]{1,0:T(8,128)(2,1)S(1)} fusion(bf16[85,4096]{1,0:T(8,128)(2,1)S(1)} %reshape.25, s32[512]{0:T(512)S(1)} %collective-permute-done.6), kind=kOutput, calls=%fused_computation.39 | convolution fusion | flops 358656512 | bytes 785408 | tf_op jit(solution)/shard_map/dot_general | solution.py:16
  25.9 1.7 %collective-permute-start.7 = (bf16[85,512]{1,0:T(8,128)(2,1)S(1)}, bf16[85,512]{1,0:T(8,128)(2,1)S(1)}, u32[]{:S(2)}, u32[]{:S(2)}) collective-permute-start(bf16[85,512]{1,0:T(8,128)(2,1)S(1)} %fusion.35), channel_id=1, source_target_pairs={{8,0},{12,4},{16,8},{20,12},{24,16},{28,20},{0,24},{4,28},{9,1},{1... | collective-permute-start | bytes 261128 | tf_op jit(solution)/shard_map/ppermute | solution.py:10
  27.7 0.0 collective-permute-done.1
  27.7 0.0 collective-permute-done.3
  27.7 1.5 %fusion.33 = bf16[5,85,512]{2,1,0:T(8,128)(2,1)S(1)} fusion(bf16[5,85,512]{2,1,0:T(8,128)(2,1)S(1)} %bitcast_dynamic-update-slice_fusion.7, bf16[85,4096]{1,0:T(8,128)(2,1)S(1)} %reshape.25, s32[512]{0:T(512)S(1)} %get-tuple-element.6), kind=kOutput, calls=%fused_computation.37 | convolution fusion | flops 358656512 | bytes 813056 | tf_op jit(solution)/shard_map/dot_general | solution.py:16
  29.2 0.0 collective-permute-done.5
  29.2 2.7 %collective-permute-done.7 = bf16[85,512]{1,0:T(8,128)(2,1)S(1)} collective-permute-done((bf16[85,512]{1,0:T(8,128)(2,1)S(1)}, bf16[85,512]{1,0:T(8,128)(2,1)S(1)}, u32[]{:S(2)}, u32[]{:S(2)}) %collective-permute-start.7) | collective-permute-done | bytes 87072 | tf_op jit(solution)/shard_map/ppermute | solution.py:10
  32.0 1.9 %convolution_convert_fusion = bf16[85,2048]{1,0:T(8,128)(2,1)S(1)} fusion(bf16[85,2560]{1,0:T(8,128)(2,1)S(1)} %bitcast_dynamic-update-slice_fusion, bf16[2560,2048]{1,0:T(8,128)(2,1)S(1)} %bitcast.54), kind=kOutput, calls=%fused_computation.26 | convolution fusion | flops 891463680 | bytes 11269120 | tf_op jit(solution)/shard_map/dot_general | solution.py:45
  33.9 0.0 copy-start
  33.9 0.0 copy-start.1
  33.9 0.1 reshape.27
  34.0 4.2 %copy.26 = bf16[5,17,2048]{1,0,2:T(8,128)(2,1)} copy(bf16[5,17,2048]{2,1,0:T(8,128)(2,1)S(1)} %reshape.27) | data formatting | bytes 696320 | tf_op jit(solution)/shard_map/reshape | solution.py:48
  38.2 5.9 %reshape.28 = bf16[4,2,21760]{2,1,0:T(2,128)(2,1)} reshape(bf16[2048,5,17]{2,1,0:T(8,128)(2,1)} %bitcast.55) | data formatting | bytes 696320
  44.2 4.9 %all-to-all-start = ((bf16[4,2,21760]{2,1,0:T(2,128)(2,1)}), bf16[4,2,21760]{2,1,0:T(2,128)(2,1)S(1)}, u32[]{:S(2)}, u32[]{:S(2)}) async-start(bf16[4,2,21760]{2,1,0:T(2,128)(2,1)} %reshape.28), calls=%async_computation | async-start | bytes 696320 | tf_op jit(solution)/shard_map/all_to_all | solution.py:55
  49.0 0.1 copy.32
  49.2 0.1 copy.30
  49.3 0.1 copy.29
  49.5 0.1 copy.31
  49.6 9.9 %all-to-all-done = bf16[4,2,21760]{2,1,0:T(2,128)(2,1)S(1)} async-done(((bf16[4,2,21760]{2,1,0:T(2,128)(2,1)}), bf16[4,2,21760]{2,1,0:T(2,128)(2,1)S(1)}, u32[]{:S(2)}, u32[]{:S(2)}) %all-to-all-start) | async-done | bytes 348192 | tf_op jit(solution)/shard_map/all_to_all | solution.py:55
  59.5 5.0 %reshape.29 = bf16[2048,5,17]{2,1,0:T(8,128)(2,1)} reshape(bf16[4,2,21760]{2,1,0:T(2,128)(2,1)S(1)} %all-to-all-done) | data formatting | bytes 696320
  64.5 4.2 %copy.35 = bf16[5,17,4,512]{3,2,1,0:T(4,128)(2,1)S(1)} copy(bf16[5,17,4,512]{1,0,3,2:T(8,128)(2,1)} %bitcast.56) | data formatting | bytes 696320 | tf_op jit(solution)/shard_map/all_to_all | solution.py:55
  68.7 0.1 copy.28
  68.8 0.1 all_to_all.16
  68.9 0.8 copy.33
  69.7 12.9 %fusion.22 = bf16[5,127,512]{1,0,2:T(8,128)(2,1)S(1)} fusion(bf16[5,68,512]{1,0,2:T(8,128)(2,1)S(1)} %copy.33, f32[127,512]{0,1:T(8,128)S(1)} %copy.32, s32[127,512]{0,1:T(8,128)S(1)} %copy.31, f32[127,512]{0,1:T(8,128)S(1)} %copy.30, s32[127,512]{0,1:T(8,128)S(1)} %copy.29), kind=kOutput, calls=%fused_computation.28 | convolution fusion | flops 287731200 | bytes 2038784 | tf_op jit(solution)/shard_map/jlc,flc->fjc/dot_general | solution.py:58
  82.6 1.4 %copy.34 = bf16[5,127,512]{2,1,0:T(8,128)(2,1)} copy(bf16[5,127,512]{1,0,2:T(8,128)(2,1)S(1)} %fusion.22) | data formatting | bytes 1300480 | tf_op jit(solution)/shard_map/convert_element_type | solution.py:59
  (17 shorter events, 0.2 us)
Async XLA Ops:
  1.5 15.6 %collective-permute-start.2 = (s32[512]{0:T(512)S(1)}, s32[512]{0:T(512)S(1)}, u32[]{:S(2)}, u32[]{:S(2)}) collective-permute-start(s32[512]{0:T(512)S(1)} %get-tuple-element.7), channel_id=1, source_target_pairs={{4,0},{8,4},{12,8},{16,12},{20,16},{24,20},{28,24},{0,28},{5,1},{9... | collective-permute-start | bytes 6152 | tf_op jit(solution)/shard_map/ppermute | solution.py:10
  1.6 18.2 %collective-permute-start = (s32[512]{0:T(512)S(1)}, s32[512]{0:T(512)S(1)}, u32[]{:S(2)}, u32[]{:S(2)}) collective-permute-start(s32[512]{0:T(512)S(1)} %get-tuple-element.8), channel_id=1, source_target_pairs={{8,0},{12,4},{16,8},{20,12},{24,16},{28,20},{0,24},{4,28},{9,1},{1... | collective-permute-start | bytes 6152 | tf_op jit(solution)/shard_map/ppermute | solution.py:10
  4.0 18.9 %collective-permute-start.4 = (s32[512]{0:T(512)S(1)}, s32[512]{0:T(512)S(1)}, u32[]{:S(2)}, u32[]{:S(2)}) collective-permute-start(s32[512]{0:T(512)S(1)} %get-tuple-element.9), channel_id=1, source_target_pairs={{28,0},{0,4},{4,8},{8,12},{12,16},{16,20},{20,24},{24,28},{29,1},{... | collective-permute-start | bytes 6152 | tf_op jit(solution)/shard_map/ppermute | solution.py:10
  4.0 20.5 %collective-permute-start.6 = (s32[512]{0:T(512)S(1)}, s32[512]{0:T(512)S(1)}, u32[]{:S(2)}, u32[]{:S(2)}) collective-permute-start(s32[512]{0:T(512)S(1)} %get-tuple-element.5), channel_id=1, source_target_pairs={{24,0},{28,4},{0,8},{4,12},{8,16},{12,20},{16,24},{20,28},{25,1},{... | collective-permute-start | bytes 6152 | tf_op jit(solution)/shard_map/ppermute | solution.py:10
  17.1 14.9 %slice-start = ((s8[10485760]{0:T(1024)(128)(4,1)}), s8[4194304]{0:T(1024)(128)(4,1)S(1)}, s32[]{:S(2)}) async-start(s8[10485760]{0:T(1024)(128)(4,1)} %bitcast.52), calls=%async_computation.1 | async-start | bytes 8388608
  18.6 13.4 %slice-start.1 = ((s8[10485760]{0:T(1024)(128)(4,1)}), s8[4194304]{0:T(1024)(128)(4,1)S(1)}, s32[]{:S(2)}) async-start(s8[10485760]{0:T(1024)(128)(4,1)} %bitcast.52), calls=%async_computation.2 | async-start | bytes 8388608
  18.6 9.1 %collective-permute-start.3 = (bf16[85,512]{1,0:T(8,128)(2,1)S(1)}, bf16[85,512]{1,0:T(8,128)(2,1)S(1)}, u32[]{:S(2)}, u32[]{:S(2)}) collective-permute-start(bf16[85,512]{1,0:T(8,128)(2,1)S(1)} %fusion.31), channel_id=1, source_target_pairs={{28,0},{0,4},{4,8},{8,12},{12,16},{16,20},{20,24},{24,28},{29,1},{... | collective-permute-start | bytes 261128 | tf_op jit(solution)/shard_map/ppermute | solution.py:10
  21.2 6.5 %collective-permute-start.1 = (bf16[85,512]{1,0:T(8,128)(2,1)S(1)}, bf16[85,512]{1,0:T(8,128)(2,1)S(1)}, u32[]{:S(2)}, u32[]{:S(2)}) collective-permute-start(bf16[85,512]{1,0:T(8,128)(2,1)S(1)} %fusion.30), channel_id=1, source_target_pairs={{24,0},{28,4},{0,8},{4,12},{8,16},{12,20},{16,24},{20,28},{25,1},{... | collective-permute-start | bytes 261128 | tf_op jit(solution)/shard_map/ppermute | solution.py:10
  24.3 7.7 %slice-start.2 = ((s8[10485760]{0:T(1024)(128)(4,1)}), s8[2097152]{0:T(1024)(128)(4,1)S(1)}, s32[]{:S(2)}) async-start(s8[10485760]{0:T(1024)(128)(4,1)} %bitcast.52), calls=%async_computation.3 | async-start | bytes 4194304
  24.3 4.8 %collective-permute-start.5 = (bf16[85,512]{1,0:T(8,128)(2,1)S(1)}, bf16[85,512]{1,0:T(8,128)(2,1)S(1)}, u32[]{:S(2)}, u32[]{:S(2)}) collective-permute-start(bf16[85,512]{1,0:T(8,128)(2,1)S(1)} %fusion.34), channel_id=1, source_target_pairs={{4,0},{8,4},{12,8},{16,12},{20,16},{24,20},{28,24},{0,28},{5,1},{9... | collective-permute-start | bytes 261128 | tf_op jit(solution)/shard_map/ppermute | solution.py:10
  25.9 5.9 %collective-permute-start.7 = (bf16[85,512]{1,0:T(8,128)(2,1)S(1)}, bf16[85,512]{1,0:T(8,128)(2,1)S(1)}, u32[]{:S(2)}, u32[]{:S(2)}) collective-permute-start(bf16[85,512]{1,0:T(8,128)(2,1)S(1)} %fusion.35), channel_id=1, source_target_pairs={{8,0},{12,4},{16,8},{20,12},{24,16},{28,20},{0,24},{4,28},{9,1},{1... | collective-permute-start | bytes 261128 | tf_op jit(solution)/shard_map/ppermute | solution.py:10
  33.9 15.1 %copy-start = (f32[127,512]{1,0:T(8,128)S(1)}, f32[127,512]{1,0:T(8,128)}, u32[]{:S(2)}) copy-start(f32[127,512]{1,0:T(8,128)} %param.11) | copy-start | bytes 780292
  33.9 15.4 %copy-start.1 = (s32[127,512]{1,0:T(8,128)S(1)}, s32[127,512]{1,0:T(8,128)}, u32[]{:S(2)}) copy-start(s32[127,512]{1,0:T(8,128)} %param.10) | copy-start | bytes 780292
  44.2 15.4 %all-to-all-start = ((bf16[4,2,21760]{2,1,0:T(2,128)(2,1)}), bf16[4,2,21760]{2,1,0:T(2,128)(2,1)S(1)}, u32[]{:S(2)}, u32[]{:S(2)}) async-start(bf16[4,2,21760]{2,1,0:T(2,128)(2,1)} %reshape.28), calls=%async_computation | async-start | bytes 696320 | tf_op jit(solution)/shard_map/all_to_all | solution.py:55
where the time goes:
time: 84.6 us; the launch traced here: 84 us
  local copies, waits for them, and re-layouts  24.5 us (29%)
  matrix products  22.2 us (26%)
  starting transfers between devices  12.7 us (15%)
  waiting for transfers between devices  12.5 us (15%)
  between operations  9.9 us (12%)
  other arithmetic  2.19 us (3%)
    dot_general x1, matrix products, local(): jnp.einsum('jlc,flc->fjc', interp, widened, precision=lax.Precision.HIGHEST)  12.9 us
    unnamed x21, local copies, waits for them, and re-layouts  11.2 us
    all_to_all x1, waiting for transfers between devices, local(): lax.all_to_all(horizontal, 'lev', split_axis=2, concat_axis=1, tiled=True)  9.87 us
    ppermute x8, starting transfers between devices, shifted(): return lax.ppermute(block, axis, route)  7.8 us
    dot_general x5, matrix products, select_cells(): jnp.dot(tile, picker, preferred_element_type=jnp.float32)  7.4 us
    all_to_all x4, local copies, waits for them, and re-layouts, local(): lax.all_to_all(horizontal, 'lev', split_axis=2, concat_axis=1, tiled=True)  5.19 us
    all_to_all x1, starting transfers between devices, local(): lax.all_to_all(horizontal, 'lev', split_axis=2, concat_axis=1, tiled=True)  4.88 us
    reshape x2, local copies, waits for them, and re-layouts, local(): horizontal = horizontal.reshape(fields, level_slab, blocks.shape[2])  4.33 us
  transfers between devices with their start and end apart: 9, of which 2 were waited for; matrix products, arithmetic and copies ran while one was open for 13% of the time, Pallas kernels for 0%

commit v1 on v0

--- a/solution.py
+++ b/solution.py
@@ -52,9 +52,10 @@
     upper_hit = level_ids == bracket[:, None, :] + 1
     upper_share = fraction[:, None, :]
     interp = jnp.where(lower_hit, 1.0 - upper_share, 0.0) + jnp.where(upper_hit, upper_share, 0.0)
-    widened = lax.all_to_all(horizontal, "lev", split_axis=2, concat_axis=1, tiled=True).astype(
-        jnp.float32
-    )
+    widened = jnp.concatenate(
+        lax.all_to_all(jnp.stack(jnp.split(horizontal, lax.axis_size("lev"), 2)), "lev", 0, 0),
+        axis=1,
+    ).astype(jnp.float32)
     mixed = jnp.einsum("jlc,flc->fjc", interp, widened, precision=lax.Precision.HIGHEST)
     return mixed.astype(jnp.bfloat16)
 

time: 84.6 us -> 68.7 us (0.81)
  local copies, waits for them, and re-layouts: 24.5 us -> 5.21 us
  waiting for transfers between devices: 12.5 us -> 14.9 us
  other arithmetic: 2.19 us -> 3.05 us
    unnamed x21 -> x19, local copies, waits for them, and re-layouts: 11.2 us -> 0.37 us
    all_to_all x4 -> x0, local copies, waits for them, and re-layouts: 5.19 us -> none  [local(): lax.all_to_all(horizontal, 'lev', split_axis=2, concat_axis=1, tiled=True)]
    reshape x2 -> x1, local copies, waits for them, and re-layouts: 4.33 us -> 0.12 us  [local(): horizontal = horizontal.reshape(fields, level_slab, blocks.shape[2])]
    all_to_all x1, waiting for transfers between devices: 9.87 us -> 11.7 us  [local(): lax.all_to_all(jnp.stack(jnp.split(horizontal, lax.axis_size('lev'), 2)),...]
    reshape x0 -> x3, local copies, waits for them, and re-layouts: none -> 0.92 us  [local(): jnp.concatenate(lax.all_to_all(jnp.stack(jnp.split(horizontal, lax.axis_s...]
    another operation x0 -> x1, other arithmetic: none -> 0.86 us  [local(): jnp.stack(jnp.split(horizontal, lax.axis_size('lev'), 2))]
  transfers between devices with their start and end apart: 9 -> 9, of which waited for: 2 -> 2; matrix products, arithmetic and copies ran while one was open for 13% -> 16% of each run, Pallas kernels for 0% -> 0%
where the time goes in v1:
time: 68.7 us; the launch traced here: 67.3 us
  matrix products  22.2 us (32%)
  waiting for transfers between devices  14.9 us (22%)
  starting transfers between devices  12.3 us (18%)
  between operations  9.73 us (14%)
  local copies, waits for them, and re-layouts  5.21 us (8%)
  other arithmetic  3.05 us (4%)
    dot_general x1, matrix products, local(): jnp.einsum('jlc,flc->fjc', interp, widened, precision=lax.Precision.HIGHEST)  12.9 us
    all_to_all x1, waiting for transfers between devices, local(): lax.all_to_all(jnp.stack(jnp.split(horizontal, lax.axis_size('lev'), 2)),...  11.7 us
    ppermute x8, starting transfers between devices, shifted(): return lax.ppermute(block, axis, route)  7.42 us
    dot_general x5, matrix products, select_cells(): jnp.dot(tile, picker, preferred_element_type=jnp.float32)  7.4 us
    all_to_all x1, starting transfers between devices, local(): lax.all_to_all(jnp.stack(jnp.split(horizontal, lax.axis_size('lev'), 2)),...  4.88 us
    ppermute x8, waiting for transfers between devices, shifted(): return lax.ppermute(block, axis, route)  3.13 us
    dot_general x1, matrix products, local(): jnp.dot(chosen, weights_flat, preferred_element_type=jnp.float32)  1.85 us
    reshape x1, local copies, waits for them, and re-layouts, local(): stacked = source_state.reshape(fields * level_slab, tile_cells)  1.45 us
  transfers between devices with their start and end apart: 9, of which 2 were waited for; matrix products, arithmetic and copies ran while one was open for 16% of the time, Pallas kernels for 0%

profile of v1, /device:TPU:2, one launch (start us, length us, event | category | flops | bytes accessed | tf_op | source)
XLA Modules:
  0.0 67.3 jit_solution(3624340371518936632)
XLA Ops:
  0.0 0.7 broadcast_compare_fusion.1
  0.7 0.8 %select_reduce_fusion = (s32[512]{0:T(512)S(1)}, s32[512]{0:T(512)S(1)}, s32[512]{0:T(512)S(1)}, s32[512]{0:T(512)S(1)}, s32[512]{0:T(512)S(1)}) fusion(s32[5,512]{1,0:T(8,128)} %param.8, pred[5]{0:T(512)(128)(4,1)S(1)} %get-tuple-element.23, pred[5]{0:T(512)(128)(4,1)S(1)} %get-tuple-element.20, pred[5]{0:T(512)(128)(4,1)S(1)} %get-tuple-element.21, ...), kind=kLoop, calls=%fused_computation.56 | loop fusion | flops 23040 | bytes 20505 | tf_op jit(solution)/shard_map/reduce_sum | solution.py:31
  1.5 1.5 %collective-permute-start.6 = (s32[512]{0:T(512)S(1)}, s32[512]{0:T(512)S(1)}, u32[]{:S(2)}, u32[]{:S(2)}) collective-permute-start(s32[512]{0:T(512)S(1)} %get-tuple-element.5), channel_id=1, source_target_pairs={{24,0},{28,4},{0,8},{4,12},{8,16},{12,20},{16,24},{20,28},{25,1},{... | collective-permute-start | bytes 6152 | tf_op jit(solution)/shard_map/ppermute | solution.py:10
  3.0 0.0 collective-permute-start.2
  3.0 1.0 %collective-permute-start = (s32[512]{0:T(512)S(1)}, s32[512]{0:T(512)S(1)}, u32[]{:S(2)}, u32[]{:S(2)}) collective-permute-start(s32[512]{0:T(512)S(1)} %get-tuple-element.8), channel_id=1, source_target_pairs={{8,0},{12,4},{16,8},{20,12},{24,16},{28,20},{0,24},{4,28},{9,1},{1... | collective-permute-start | bytes 6152 | tf_op jit(solution)/shard_map/ppermute | solution.py:10
  4.0 0.0 collective-permute-start.4
  4.0 0.7 and_select_fusion
  4.7 0.7 fusion.38
  11.7 1.4 %reshape.31 = bf16[85,4096]{1,0:T(8,128)(2,1)S(1)} reshape(bf16[5,17,4096]{2,1,0:T(8,128)(2,1)} %param.6) | data formatting | bytes 1392640 | tf_op jit(solution)/shard_map/reshape | solution.py:21
  16.3 0.0 collective-permute-done
  16.3 0.0 slice-start
  16.3 1.5 %fusion.30 = bf16[85,512]{1,0:T(8,128)(2,1)S(1)} fusion(bf16[85,4096]{1,0:T(8,128)(2,1)S(1)} %reshape.31, s32[512]{0:T(512)S(1)} %collective-permute-done), kind=kOutput, calls=%fused_computation.34 | convolution fusion | flops 358656512 | bytes 785408 | tf_op jit(solution)/shard_map/dot_general | solution.py:16
  17.8 0.0 slice-start.1
  17.8 2.2 %collective-permute-start.1 = (bf16[85,512]{1,0:T(8,128)(2,1)S(1)}, bf16[85,512]{1,0:T(8,128)(2,1)S(1)}, u32[]{:S(2)}, u32[]{:S(2)}) collective-permute-start(bf16[85,512]{1,0:T(8,128)(2,1)S(1)} %fusion.30), channel_id=1, source_target_pairs={{24,0},{28,4},{0,8},{4,12},{8,16},{12,20},{16,24},{20,28},{25,1},{... | collective-permute-start | bytes 261128 | tf_op jit(solution)/shard_map/ppermute | solution.py:10
  20.0 0.0 collective-permute-done.2
  20.0 1.5 %fusion.31 = bf16[85,512]{1,0:T(8,128)(2,1)S(1)} fusion(bf16[85,4096]{1,0:T(8,128)(2,1)S(1)} %reshape.31, s32[512]{0:T(512)S(1)} %collective-permute-done.2), kind=kOutput, calls=%fused_computation.35 | convolution fusion | flops 358656512 | bytes 785408 | tf_op jit(solution)/shard_map/dot_general | solution.py:16
  21.5 0.8 %collective-permute-start.3 = (bf16[85,512]{1,0:T(8,128)(2,1)S(1)}, bf16[85,512]{1,0:T(8,128)(2,1)S(1)}, u32[]{:S(2)}, u32[]{:S(2)}) collective-permute-start(bf16[85,512]{1,0:T(8,128)(2,1)S(1)} %fusion.31), channel_id=1, source_target_pairs={{28,0},{0,4},{4,8},{8,12},{12,16},{16,20},{20,24},{24,28},{29,1},{... | collective-permute-start | bytes 261128 | tf_op jit(solution)/shard_map/ppermute | solution.py:10
  22.3 0.0 collective-permute-done.4
  22.3 1.5 %fusion.34 = bf16[85,512]{1,0:T(8,128)(2,1)S(1)} fusion(bf16[85,4096]{1,0:T(8,128)(2,1)S(1)} %reshape.31, s32[512]{0:T(512)S(1)} %collective-permute-done.4), kind=kOutput, calls=%fused_computation.38 | convolution fusion | flops 358656512 | bytes 785408 | tf_op jit(solution)/shard_map/dot_general | solution.py:16
  23.8 0.0 slice-start.2
  23.8 1.0 %collective-permute-start.5 = (bf16[85,512]{1,0:T(8,128)(2,1)S(1)}, bf16[85,512]{1,0:T(8,128)(2,1)S(1)}, u32[]{:S(2)}, u32[]{:S(2)}) collective-permute-start(bf16[85,512]{1,0:T(8,128)(2,1)S(1)} %fusion.34), channel_id=1, source_target_pairs={{4,0},{8,4},{12,8},{16,12},{20,16},{24,20},{28,24},{0,28},{5,1},{9... | collective-permute-start | bytes 261128 | tf_op jit(solution)/shard_map/ppermute | solution.py:10
  24.8 0.0 collective-permute-done.6
  24.8 1.5 %fusion.35 = bf16[85,512]{1,0:T(8,128)(2,1)S(1)} fusion(bf16[85,4096]{1,0:T(8,128)(2,1)S(1)} %reshape.31, s32[512]{0:T(512)S(1)} %collective-permute-done.6), kind=kOutput, calls=%fused_computation.39 | convolution fusion | flops 358656512 | bytes 785408 | tf_op jit(solution)/shard_map/dot_general | solution.py:16
  26.3 0.8 %collective-permute-start.7 = (bf16[85,512]{1,0:T(8,128)(2,1)S(1)}, bf16[85,512]{1,0:T(8,128)(2,1)S(1)}, u32[]{:S(2)}, u32[]{:S(2)}) collective-permute-start(bf16[85,512]{1,0:T(8,128)(2,1)S(1)} %fusion.35), channel_id=1, source_target_pairs={{8,0},{12,4},{16,8},{20,12},{24,16},{28,20},{0,24},{4,28},{9,1},{1... | collective-permute-start | bytes 261128 | tf_op jit(solution)/shard_map/ppermute | solution.py:10
  27.1 0.0 collective-permute-done.1
  27.1 0.0 collective-permute-done.3
  27.2 1.5 %fusion.33 = bf16[5,85,512]{2,1,0:T(8,128)(2,1)S(1)} fusion(bf16[5,85,512]{2,1,0:T(8,128)(2,1)S(1)} %bitcast_dynamic-update-slice_fusion.7, bf16[85,4096]{1,0:T(8,128)(2,1)S(1)} %reshape.31, s32[512]{0:T(512)S(1)} %get-tuple-element.6), kind=kOutput, calls=%fused_computation.37 | convolution fusion | flops 358656512 | bytes 813056 | tf_op jit(solution)/shard_map/dot_general | solution.py:16
  28.6 0.0 collective-permute-done.5
  28.7 3.1 %collective-permute-done.7 = bf16[85,512]{1,0:T(8,128)(2,1)S(1)} collective-permute-done((bf16[85,512]{1,0:T(8,128)(2,1)S(1)}, bf16[85,512]{1,0:T(8,128)(2,1)S(1)}, u32[]{:S(2)}, u32[]{:S(2)}) %collective-permute-start.7) | collective-permute-done | bytes 87072 | tf_op jit(solution)/shard_map/ppermute | solution.py:10
  31.9 0.0 slice-done
  31.9 0.0 slice-done.1
  31.9 0.0 slice-done.2
  31.9 0.0 copy-start
  31.9 0.0 copy-start.1
  32.0 1.9 %convolution_convert_fusion = bf16[85,2048]{1,0:T(8,128)(2,1)S(1)} fusion(bf16[85,2560]{1,0:T(8,128)(2,1)S(1)} %bitcast_dynamic-update-slice_fusion, bf16[2560,2048]{1,0:T(8,128)(2,1)S(1)} %bitcast.59), kind=kOutput, calls=%fused_computation.26 | convolution fusion | flops 891463680 | bytes 11269120 | tf_op jit(solution)/shard_map/dot_general | solution.py:45
  33.8 0.1 reshape.33
  34.0 0.9 %pad_maximum_fusion = bf16[4,5,17,512]{3,2,1,0:T(8,128)(2,1)} fusion(bf16[1,5,17,512]{3,2,1,0:T(8,128)(2,1)S(1)} %get-tuple-element.11, bf16[1,5,17,512]{3,2,1,0:T(8,128)(2,1)S(1)} %get-tuple-element.12, bf16[1,5,17,512]{3,2,1,0:T(8,128)(2,1)S(1)} %get-tuple-element.13, bf16[1,5,17,512]{3,2,1,0:T(8,128)(2,1)S(1)} %get-tuple-element.10), kind=kLoop, calls=%fused_computation.40 | loop fusion | flops 522240 | bytes 696320 | tf_op jit(solution)/shard_map/stack | solution.py:56
  34.8 4.9 %all-to-all-start = ((bf16[4,5,17,512]{3,2,1,0:T(8,128)(2,1)}), bf16[4,5,17,512]{3,2,1,0:T(8,128)(2,1)S(1)}, u32[]{:S(2)}, u32[]{:S(2)}) async-start(bf16[4,5,17,512]{3,2,1,0:T(8,128)(2,1)} %pad_maximum_fusion), calls=%async_computation | async-start | bytes 983040 | tf_op jit(solution)/shard_map/all_to_all | solution.py:56
  39.7 0.0 copy-done
  39.7 0.1 copy.23
  39.9 0.1 copy.25
  40.0 0.1 copy.26
  40.2 0.1 copy.24
  40.3 11.7 %all-to-all-done = bf16[4,5,17,512]{3,2,1,0:T(8,128)(2,1)S(1)} async-done(((bf16[4,5,17,512]{3,2,1,0:T(8,128)(2,1)}), bf16[4,5,17,512]{3,2,1,0:T(8,128)(2,1)S(1)}, u32[]{:S(2)}, u32[]{:S(2)}) %all-to-all-start) | async-done | bytes 348192 | tf_op jit(solution)/shard_map/all_to_all | solution.py:56
  52.1 0.1 reshape.35
  52.3 0.8 %copy.27 = bf16[5,68,512]{1,0,2:T(8,128)(2,1)S(1)} copy(bf16[5,68,512]{2,1,0:T(8,128)(2,1)S(1)} %reshape.35) | data formatting | bytes 696320 | tf_op jit(solution)/shard_map/reshape | solution.py:55
  53.0 12.9 %fusion.22 = bf16[5,127,512]{1,0,2:T(8,128)(2,1)S(1)} fusion(bf16[5,68,512]{1,0,2:T(8,128)(2,1)S(1)} %copy.27, f32[127,512]{0,1:T(8,128)S(1)} %copy.26, s32[127,512]{0,1:T(8,128)S(1)} %copy.25, f32[127,512]{0,1:T(8,128)S(1)} %copy.24, s32[127,512]{0,1:T(8,128)S(1)} %copy.23), kind=kOutput, calls=%fused_computation.28 | convolution fusion | flops 287731200 | bytes 2038784 | tf_op jit(solution)/shard_map/jlc,flc->fjc/dot_general | solution.py:59
  66.0 1.4 %copy.28 = bf16[5,127,512]{2,1,0:T(8,128)(2,1)} copy(bf16[5,127,512]{1,0,2:T(8,128)(2,1)S(1)} %fusion.22) | data formatting | bytes 1300480 | tf_op jit(solution)/shard_map/convert_element_type | solution.py:60
  (15 shorter events, 0.2 us)
Async XLA Ops:
  1.5 23.3 %collective-permute-start.6 = (s32[512]{0:T(512)S(1)}, s32[512]{0:T(512)S(1)}, u32[]{:S(2)}, u32[]{:S(2)}) collective-permute-start(s32[512]{0:T(512)S(1)} %get-tuple-element.5), channel_id=1, source_target_pairs={{24,0},{28,4},{0,8},{4,12},{8,16},{12,20},{16,24},{20,28},{25,1},{... | collective-permute-start | bytes 6152 | tf_op jit(solution)/shard_map/ppermute | solution.py:10
  3.0 17.0 %collective-permute-start.2 = (s32[512]{0:T(512)S(1)}, s32[512]{0:T(512)S(1)}, u32[]{:S(2)}, u32[]{:S(2)}) collective-permute-start(s32[512]{0:T(512)S(1)} %get-tuple-element.7), channel_id=1, source_target_pairs={{4,0},{8,4},{12,8},{16,12},{20,16},{24,20},{28,24},{0,28},{5,1},{9... | collective-permute-start | bytes 6152 | tf_op jit(solution)/shard_map/ppermute | solution.py:10
  3.0 13.2 %collective-permute-start = (s32[512]{0:T(512)S(1)}, s32[512]{0:T(512)S(1)}, u32[]{:S(2)}, u32[]{:S(2)}) collective-permute-start(s32[512]{0:T(512)S(1)} %get-tuple-element.8), channel_id=1, source_target_pairs={{8,0},{12,4},{16,8},{20,12},{24,16},{28,20},{0,24},{4,28},{9,1},{1... | collective-permute-start | bytes 6152 | tf_op jit(solution)/shard_map/ppermute | solution.py:10
  4.0 18.3 %collective-permute-start.4 = (s32[512]{0:T(512)S(1)}, s32[512]{0:T(512)S(1)}, u32[]{:S(2)}, u32[]{:S(2)}) collective-permute-start(s32[512]{0:T(512)S(1)} %get-tuple-element.9), channel_id=1, source_target_pairs={{28,0},{0,4},{4,8},{8,12},{12,16},{16,20},{20,24},{24,28},{29,1},{... | collective-permute-start | bytes 6152 | tf_op jit(solution)/shard_map/ppermute | solution.py:10
  16.3 15.6 %slice-start = ((s8[10485760]{0:T(1024)(128)(4,1)}), s8[4194304]{0:T(1024)(128)(4,1)S(1)}, s32[]{:S(2)}) async-start(s8[10485760]{0:T(1024)(128)(4,1)} %bitcast.57), calls=%async_computation.1 | async-start | bytes 8388608
  17.8 14.1 %slice-start.1 = ((s8[10485760]{0:T(1024)(128)(4,1)}), s8[4194304]{0:T(1024)(128)(4,1)S(1)}, s32[]{:S(2)}) async-start(s8[10485760]{0:T(1024)(128)(4,1)} %bitcast.57), calls=%async_computation.2 | async-start | bytes 8388608
  17.8 9.3 %collective-permute-start.1 = (bf16[85,512]{1,0:T(8,128)(2,1)S(1)}, bf16[85,512]{1,0:T(8,128)(2,1)S(1)}, u32[]{:S(2)}, u32[]{:S(2)}) collective-permute-start(bf16[85,512]{1,0:T(8,128)(2,1)S(1)} %fusion.30), channel_id=1, source_target_pairs={{24,0},{28,4},{0,8},{4,12},{8,16},{12,20},{16,24},{20,28},{25,1},{... | collective-permute-start | bytes 261128 | tf_op jit(solution)/shard_map/ppermute | solution.py:10
  21.5 5.7 %collective-permute-start.3 = (bf16[85,512]{1,0:T(8,128)(2,1)S(1)}, bf16[85,512]{1,0:T(8,128)(2,1)S(1)}, u32[]{:S(2)}, u32[]{:S(2)}) collective-permute-start(bf16[85,512]{1,0:T(8,128)(2,1)S(1)} %fusion.31), channel_id=1, source_target_pairs={{28,0},{0,4},{4,8},{8,12},{12,16},{16,20},{20,24},{24,28},{29,1},{... | collective-permute-start | bytes 261128 | tf_op jit(solution)/shard_map/ppermute | solution.py:10
  23.8 8.1 %slice-start.2 = ((s8[10485760]{0:T(1024)(128)(4,1)}), s8[2097152]{0:T(1024)(128)(4,1)S(1)}, s32[]{:S(2)}) async-start(s8[10485760]{0:T(1024)(128)(4,1)} %bitcast.57), calls=%async_computation.3 | async-start | bytes 4194304
  23.8 4.8 %collective-permute-start.5 = (bf16[85,512]{1,0:T(8,128)(2,1)S(1)}, bf16[85,512]{1,0:T(8,128)(2,1)S(1)}, u32[]{:S(2)}, u32[]{:S(2)}) collective-permute-start(bf16[85,512]{1,0:T(8,128)(2,1)S(1)} %fusion.34), channel_id=1, source_target_pairs={{4,0},{8,4},{12,8},{16,12},{20,16},{24,20},{28,24},{0,28},{5,1},{9... | collective-permute-start | bytes 261128 | tf_op jit(solution)/shard_map/ppermute | solution.py:10
  26.3 5.5 %collective-permute-start.7 = (bf16[85,512]{1,0:T(8,128)(2,1)S(1)}, bf16[85,512]{1,0:T(8,128)(2,1)S(1)}, u32[]{:S(2)}, u32[]{:S(2)}) collective-permute-start(bf16[85,512]{1,0:T(8,128)(2,1)S(1)} %fusion.35), channel_id=1, source_target_pairs={{8,0},{12,4},{16,8},{20,12},{24,16},{28,20},{0,24},{4,28},{9,1},{1... | collective-permute-start | bytes 261128 | tf_op jit(solution)/shard_map/ppermute | solution.py:10
  31.9 7.8 %copy-start = (s32[127,512]{1,0:T(8,128)S(1)}, s32[127,512]{1,0:T(8,128)}, u32[]{:S(2)}) copy-start(s32[127,512]{1,0:T(8,128)} %param.10) | copy-start | bytes 780292
  31.9 8.1 %copy-start.1 = (f32[127,512]{1,0:T(8,128)S(1)}, f32[127,512]{1,0:T(8,128)}, u32[]{:S(2)}) copy-start(f32[127,512]{1,0:T(8,128)} %param.11) | copy-start | bytes 780292
  34.8 17.2 %all-to-all-start = ((bf16[4,5,17,512]{3,2,1,0:T(8,128)(2,1)}), bf16[4,5,17,512]{3,2,1,0:T(8,128)(2,1)S(1)}, u32[]{:S(2)}, u32[]{:S(2)}) async-start(bf16[4,5,17,512]{3,2,1,0:T(8,128)(2,1)} %pad_maximum_fusion), calls=%async_computation | async-start | bytes 983040 | tf_op jit(solution)/shard_map/all_to_all | solution.py:56
